TPU v7x, 32 devices: a whole 2x2x4 slice. The times are simulated.
32 devices in a mesh: dp: 2 (over x), mp: 16 (over z, y, core).
Axes of the slice: x: 2, y: 2, z: 4, core: 2. Of those that a mesh axis runs over, the one named last changes fastest.
Arguments:
- base_rows: bfloat16 [256, 8192], P('dp', 'mp'), may hold values from -6 to 6
- layer_rows: bfloat16 [256, 8192], P('dp', 'mp'), may hold values from -6 to 6
- cross_weight: bfloat16 [8192, 8192], P(None, 'mp'), may hold values from -0.0625 to 0.0625
- cross_bias: float32 [8192], P('mp'), may hold values from -3 to 3
- upstream: bfloat16 [256, 8192], P('dp', 'mp'), may hold values from -6 to 6
Outputs:
- crossed: bfloat16 [256, 8192], P('dp', 'mp')
- grad_base: bfloat16 [256, 8192], P('dp', 'mp')
- grad_layer: bfloat16 [256, 8192], P('dp', 'mp')
- grad_weight: float32 [8192, 8192], P('dp', 'mp')
- grad_bias: float32 [8192], P('mp')
All inputs are finite; a program needn't handle non-finite values.
Results may differ from a plain program's by a relative error of at most 0.0041.
Values may be sent and summed in bfloat16 or wider, within the bound.
No kernel may reach another device: no remote copies, remote signals or barrier semaphores. Data moves between devices by JAX's collectives and lax.ppermute only.
A program may use at most 128 MiB of HBM per device.

v0:
```python
import jax
import jax.numpy as jnp
from jax import lax
from jax.sharding import PartitionSpec as P


def local(base_rows, layer_rows, cross_weight, cross_bias, upstream):
    groups = lax.axis_size("dp")
    row_block = lax.all_to_all(cross_weight, "mp", split_axis=0, concat_axis=1, tiled=True)
    full_rows = lax.all_gather(layer_rows, "mp", axis=1, tiled=True)
    mixed = jnp.dot(full_rows, cross_weight, preferred_element_type=jnp.float32) + cross_bias
    base = base_rows.astype(jnp.float32)
    crossed = (base * mixed + layer_rows.astype(jnp.float32)).astype(jnp.bfloat16)
    upper = upstream.astype(jnp.float32)
    delta = upper * base
    delta_low = delta.astype(jnp.bfloat16)
    grad_base = (upper * mixed).astype(jnp.bfloat16)
    back = lax.dot_general(
        lax.all_gather(delta_low, "mp", axis=1, tiled=True),
        row_block,
        (((1,), (1,)), ((), ())),
        preferred_element_type=jnp.float32,
    )
    grad_layer = (upper + back).astype(jnp.bfloat16)
    scale = jnp.float32(base_rows.shape[0] * groups) ** (-0.5)
    grad_weight = (
        lax.psum_scatter(
            lax.dot_general(
                full_rows, delta_low, (((0,), (0,)), ((), ())), preferred_element_type=jnp.float32
            ),
            "dp",
            scatter_dimension=0,
            tiled=True,
        )
        * scale
    )
    grad_bias = lax.psum(jnp.sum(delta, axis=0), "dp") * scale
    return (crossed, grad_base, grad_layer, grad_weight, grad_bias)


def solution(mesh):
    return jax.shard_map(
        local,
        mesh=mesh,
        in_specs=(P("dp", "mp"), P("dp", "mp"), P(None, "mp"), P("mp"), P("dp", "mp")),
        out_specs=(P("dp", "mp"), P("dp", "mp"), P("dp", "mp"), P("dp", "mp"), P("mp")),
        check_vma=False,
    )
```

profile of v0, /device:TPU:0, one launch (start us, length us, event | category | flops | bytes accessed | tf_op | source)
XLA Modules:
  0.0 428.7 jit_solution(16000133492980373238)
XLA Ops:
  7.2 0.0 all-gather.3.cloned.1.call-start
  7.2 0.7 all-gather.3.cloned.1.call-update
  7.9 0.0 all-gather.5.cloned.1.call-start
  7.9 46.0 %all-gather.3.cloned.1.call-done = bf16[128,8192]{1,0:T(8,128)(2,1)} async-done(((bf16[128,512]{1,0:T(8,128)(2,1)}), bf16[128,8192]{1,0:T(8,128)(2,1)}) %all-gather.3.cloned.1.call-update) | async-done | bytes 2097168 | tf_op jit(solution)/shard_map/all_gather | solution.py:10
  53.9 0.0 copy-start
  53.9 6.2 %fusion.3 = (bf16[128,512]{1,0:T(8,128)(2,1)}, bf16[128,512]{1,0:T(8,128)(2,1)}, bf16[128,512]{1,0:T(8,128)(2,1)}, f32[512]{0:T(512)S(1)}) fusion(bf16[128,512]{1,0:T(8,128)(2,1)} %param.9, bf16[128,512]{1,0:T(8,128)(2,1)} %param.6, bf16[128,512]{1,0:T(8,128)(2,1)} %param.5, f32[512]{0:T(512)} %param.8, bf16[128,8192]{1,0:T(8,128)(2,1)} %all-gather.3.cloned.1.call-done, ...), kind=kOutput, calls=%fused_computation.10 | convolution fusion | flops 1074527744 | bytes 11276288 | tf_op jit(solution)/shard_map/dot_general | solution.py:11
  60.1 0.0 all-gather.5.cloned.1.call-update
  60.2 0.0 reduce-scatter.2.cloned.1.call-start
  60.2 0.0 copy-done
  60.2 9.0 %convolution_bitcast_fusion = f32[8192,512]{0,1:T(8,128)} fusion(bf16[128,512]{1,0:T(8,128)(2,1)} %get-tuple-element.24, bf16[128,8192]{1,0:T(8,128)(2,1)S(1)} %copy-done), kind=kOutput, calls=%fused_computation | convolution fusion | flops 1073741824 | bytes 19005440 | tf_op jit(solution)/shard_map/dot_general | solution.py:28
  69.2 0.0 reduce-scatter.2.cloned.1.call-update
  69.2 4.8 %all-to-all-start = ((bf16[16,512,512]{2,1,0:T(8,128)(2,1)}), bf16[16,512,512]{2,1,0:T(8,128)(2,1)}, u32[]{:S(2)}, u32[]{:S(2)}) async-start(bf16[16,512,512]{2,1,0:T(8,128)(2,1)} %bitcast.12), calls=%async_computation | async-start | bytes 16777216 | tf_op jit(solution)/shard_map/all_to_all | solution.py:9
  74.0 4.9 %psum.7 = f32[512]{0:T(512)S(1)} all-reduce(f32[512]{0:T(512)S(1)} %get-tuple-element.25), channel_id=1, replica_groups=mesh['dp'=2,'mp'=16] {'dp'}, use_global_device_ids=true, to_apply=%region_2.0 | all-reduce | flops 512 | bytes 4096 | tf_op jit(solution)/shard_map/psum | solution.py:37
  79.0 0.6 broadcast_multiply_fusion.1
  79.6 154.0 %all-to-all-done = bf16[16,512,512]{2,1,0:T(8,128)(2,1)} async-done(((bf16[16,512,512]{2,1,0:T(8,128)(2,1)}), bf16[16,512,512]{2,1,0:T(8,128)(2,1)}, u32[]{:S(2)}, u32[]{:S(2)}) %all-to-all-start) | async-done | bytes 8388640 | tf_op jit(solution)/shard_map/all_to_all | solution.py:9
  233.6 0.0 copy-start.1
  233.6 12.3 %copy.12 = bf16[512,16,512]{0,2,1:T(8,128)(2,1)} copy(bf16[512,16,512]{2,0,1:T(8,128)(2,1)} %bitcast.1) | data formatting | bytes 16777216 | tf_op jit(solution)/shard_map/all_to_all | solution.py:9
  245.9 0.0 all-gather.5.cloned.1.call-done
  245.9 0.0 copy-done.1
  245.9 6.2 %fusion = bf16[128,512]{1,0:T(8,128)(2,1)} fusion(bf16[128,8192]{1,0:T(8,128)(2,1)} %all-gather.5.cloned.1.call-done, bf16[512,8192]{0,1:T(8,128)(2,1)} %bitcast.11, bf16[128,512]{1,0:T(8,128)(2,1)S(1)} %copy-done.1), kind=kOutput, calls=%fused_computation.4 | convolution fusion | flops 1073938432 | bytes 10747904 | tf_op jit(solution)/shard_map/dot_general | solution.py:18
  252.1 153.4 %reduce-scatter.2.cloned.1.call-done = f32[4096,512]{0,1:T(8,128)} async-done(((f32[8192,512]{0,1:T(8,128)}), f32[4096,512]{0,1:T(8,128)}) %reduce-scatter.2.cloned.1.call-update) | async-done | bytes 8388624 | tf_op jit(solution)/shard_map/reduce_scatter | solution.py:27
  405.5 7.8 %broadcast_multiply_fusion = f32[4096,512]{0,1:T(8,128)} fusion(f32[4096,512]{0,1:T(8,128)} %reduce-scatter.2.cloned.1.call-done), kind=kLoop, calls=%fused_computation.1 | loop fusion | flops 2097152 | bytes 16777216 | tf_op jit(solution)/shard_map/mul | solution.py:27
  413.3 8.9 %copy.13 = f32[4096,512]{1,0:T(8,128)} copy(f32[4096,512]{0,1:T(8,128)} %broadcast_multiply_fusion) | data formatting | bytes 16777216
Async XLA Ops:
  7.2 46.8 %all-gather.3.cloned.1.call-start = ((), (), s32[]{:S(2)}) async-start(), calls=%async_computation.2 | async-start | bytes 2228224 | tf_op jit(solution)/shard_map/all_gather | solution.py:10
  7.9 238.0 %all-gather.5.cloned.1.call-start = ((), (), s32[]{:S(2)}) async-start(), calls=%async_computation.3 | async-start | bytes 2228224 | tf_op jit(solution)/shard_map/all_gather | solution.py:19
  53.9 6.3 %copy-start = (bf16[128,8192]{1,0:T(8,128)(2,1)S(1)}, bf16[128,8192]{1,0:T(8,128)(2,1)}, u32[]{:S(2)}) copy-start(bf16[128,8192]{1,0:T(8,128)(2,1)} %all-gather.3.cloned.1.call-done) | copy-start | bytes 6291460
  60.2 345.3 %reduce-scatter.2.cloned.1.call-start = ((), (), s32[]{:S(2)}) async-start(), calls=%async_computation.4 | async-start | bytes 25165824 | tf_op jit(solution)/shard_map/reduce_scatter | solution.py:27
  69.2 164.3 %all-to-all-start = ((bf16[16,512,512]{2,1,0:T(8,128)(2,1)}), bf16[16,512,512]{2,1,0:T(8,128)(2,1)}, u32[]{:S(2)}, u32[]{:S(2)}) async-start(bf16[16,512,512]{2,1,0:T(8,128)(2,1)} %bitcast.12), calls=%async_computation | async-start | bytes 16777216 | tf_op jit(solution)/shard_map/all_to_all | solution.py:9
  233.6 12.3 %copy-start.1 = (bf16[128,512]{1,0:T(8,128)(2,1)S(1)}, bf16[128,512]{1,0:T(8,128)(2,1)}, u32[]{:S(2)}) copy-start(bf16[128,512]{1,0:T(8,128)(2,1)} %param.9) | copy-start | bytes 393220
Sparse Core Ops, SparseCore 0:
  10.1 43.7 all-gather.2
  60.3 143.4 all-gather.4
  206.1 199.3 reduce-scatter.1
where the time goes:
time: 429 us
  waiting for transfers between devices  354 us (83%)
  matrix products  21.4 us (5%)
  local copies, waits for them, and re-layouts  21.3 us (5%)
  between operations  13.8 us (3%)
  other arithmetic  8.35 us (2%)
  blocking collectives  4.93 us (1%)
  starting transfers between devices  4.92 us (1%)
    all_to_all x1, waiting for transfers between devices, local(): lax.all_to_all(cross_weight, 'mp', split_axis=0, concat_axis=1, tiled=True)  154 us
    reduce_scatter x1, waiting for transfers between devices, local(): lax.psum_scatter(lax.dot_general(full_rows, delta_low, (((0,), (0,)), (()...  153 us
    all_gather x1, waiting for transfers between devices, local(): full_rows = lax.all_gather(layer_rows, 'mp', axis=1, tiled=True)  46 us
    all_to_all x1, local copies, waits for them, and re-layouts, local(): lax.all_to_all(cross_weight, 'mp', split_axis=0, concat_axis=1, tiled=True)  12.3 us
    dot_general x1, matrix products, local(): lax.dot_general(full_rows, delta_low, (((0,), (0,)), ((), ())), preferred...  8.99 us
    unnamed x5, local copies, waits for them, and re-layouts  8.95 us
  transfers between devices with their start and end apart: 4, of which 3 were waited for; matrix products, arithmetic and copies ran while one was open for 7% of the time, Pallas kernels for 0%

commit v1 on v0

--- a/solution.py
+++ b/solution.py
@@ -7,7 +7,14 @@
 def local(base_rows, layer_rows, cross_weight, cross_bias, upstream):
     groups = lax.axis_size("dp")
     row_block = lax.all_to_all(cross_weight, "mp", split_axis=0, concat_axis=1, tiled=True)
-    full_rows = lax.all_gather(layer_rows, "mp", axis=1, tiled=True)
+    count = lax.axis_size("mp")
+    route = [(i, (i + 1) % count) for i in range(count)]
+    pieces = [layer_rows]
+    for far in range(1, count):
+        pieces = [lax.ppermute(pieces[0], "mp", route), *pieces]
+    result = jnp.concatenate(pieces, axis=1)
+    shift = (lax.axis_index("mp") + 1) * pieces[-1].shape[1]
+    full_rows = jnp.roll(result, shift, axis=1)
     mixed = jnp.dot(full_rows, cross_weight, preferred_element_type=jnp.float32) + cross_bias
     base = base_rows.astype(jnp.float32)
     crossed = (base * mixed + layer_rows.astype(jnp.float32)).astype(jnp.bfloat16)

time: 429 us -> 363 us (0.85)
  the two profiles are of different devices: /device:TPU:0 before, /device:TPU:15 now
where the time goes in v1:
time: 363 us
  waiting for transfers between devices  215 us (59%)
  starting transfers between devices  82.4 us (23%)
  matrix products  22.8 us (6%)
  between operations  15.8 us (4%)
  local copies, waits for them, and re-layouts  13.5 us (4%)
  other arithmetic  8.4 us (2%)
  blocking collectives  4.38 us (1%)
    all_to_all x1, waiting for transfers between devices, local(): lax.all_to_all(cross_weight, 'mp', split_axis=0, concat_axis=1, tiled=True)  186 us
    ppermute x15, starting transfers between devices, local(): pieces = [lax.ppermute(pieces[0], 'mp', route), *pieces]  48.6 us
    all_to_all x1, starting transfers between devices, local(): lax.all_to_all(cross_weight, 'mp', split_axis=0, concat_axis=1, tiled=True)  33.8 us
    ppermute x15, waiting for transfers between devices, local(): pieces = [lax.ppermute(pieces[0], 'mp', route), *pieces]  29.5 us
    all_to_all x1, local copies, waits for them, and re-layouts, local(): lax.all_to_all(cross_weight, 'mp', split_axis=0, concat_axis=1, tiled=True)  12.3 us
    dot_general x1, matrix products, local(): lax.dot_general(full_rows, delta_low, (((0,), (0,)), ((), ())), preferred...  9.71 us
    mul x1, other arithmetic, local(): lax.psum_scatter(lax.dot_general(full_rows, delta_low, (((0,), (0,)), (()...  7.82 us
  transfers between devices with their start and end apart: 18, of which 16 were waited for; matrix products, arithmetic and copies ran while one was open for 8% of the time, Pallas kernels for 0%

profile of v1, /device:TPU:15, one launch (start us, length us, event | category | flops | bytes accessed | tf_op | source)
XLA Modules:
  0.0 362.7 jit_solution(10095807290129316166)
XLA Ops:
  8.0 0.0 copy-start.1
  8.0 0.0 all-gather.2.cloned.1.call-start
  8.1 1.9 collective-permute-start
  9.9 2.3 collective-permute-done
  12.2 3.2 collective-permute-start.1
  15.4 1.9 collective-permute-done.1
  17.4 3.3 collective-permute-start.2
  20.7 1.9 collective-permute-done.2
  22.7 3.3 collective-permute-start.3
  26.0 1.9 collective-permute-done.3
  27.9 3.3 collective-permute-start.4
  31.3 1.9 collective-permute-done.4
  33.2 3.3 collective-permute-start.5
  36.6 1.9 collective-permute-done.5
  38.5 3.3 collective-permute-start.6
  41.9 1.9 collective-permute-done.6
  43.8 3.3 collective-permute-start.7
  47.2 1.9 collective-permute-done.7
  49.1 3.3 collective-permute-start.8
  52.5 1.9 collective-permute-done.8
  54.4 3.3 collective-permute-start.9
  57.8 1.9 collective-permute-done.9
  59.7 3.3 collective-permute-start.10
  63.0 1.9 collective-permute-done.10
  65.0 3.3 collective-permute-start.11
  68.3 1.9 collective-permute-done.11
  70.3 3.3 collective-permute-start.12
  73.6 1.9 collective-permute-done.12
  75.6 3.3 collective-permute-start.13
  78.9 1.9 collective-permute-done.13
  80.9 3.3 collective-permute-start.14
  84.2 1.9 collective-permute-done.14
  86.4 0.9 constant_dynamic-update-slice_fusion.16
  87.7 0.0 copy-done.2
  87.7 0.0 copy-done.3
  87.7 0.0 copy-start
  87.7 7.1 %fusion.10 = (bf16[128,512]{1,0:T(8,128)(2,1)}, bf16[128,512]{1,0:T(8,128)(2,1)}, bf16[128,512]{1,0:T(8,128)(2,1)}, f32[512]{0:T(512)S(1)}) fusion(bf16[128,512]{1,0:T(8,128)(2,1)S(1)} %copy-done.2, bf16[128,512]{1,0:T(8,128)(2,1)S(1)} %copy-done.1, bf16[128,512]{1,0:T(8,128)(2,1)S(1)} %copy-done.3, f32[512]{0:T(512)S(1)} %copy-done.4, ...), kind=kOutput, calls=%fused_computation.13 | convolution fusion | flops 1074527744 | bytes 11276292 | tf_op jit(solution)/shard_map/dot_general | solution.py:18
  94.9 0.0 all-gather.2.cloned.1.call-update
  94.9 0.0 reduce-scatter.2.cloned.1.call-start
  94.9 9.7 %fusion = f32[8192,512]{1,0:T(8,128)} fusion(bf16[128,512]{1,0:T(8,128)(2,1)} %get-tuple-element.9, bf16[128,16384]{1,0:T(8,128)(2,1)} %copy-done, s32[]{:T(128)S(6)} %select_n.14), kind=kOutput, calls=%fused_computation.1 | convolution fusion | flops 1073741824 | bytes 19005444 | tf_op jit(solution)/shard_map/dot_general | solution.py:35
  104.6 0.0 reduce-scatter.2.cloned.1.call-update
  104.7 33.8 %all-to-all-start = ((bf16[16,512,512]{2,1,0:T(8,128)(2,1)}), bf16[16,512,512]{2,1,0:T(8,128)(2,1)}, u32[]{:S(2)}, u32[]{:S(2)}) async-start(bf16[16,512,512]{2,1,0:T(8,128)(2,1)} %bitcast.7), calls=%async_computation | async-start | bytes 16777216 | tf_op jit(solution)/shard_map/all_to_all | solution.py:9
  138.4 4.4 %psum.7 = f32[512]{0:T(512)S(1)} all-reduce(f32[512]{0:T(512)S(1)} %get-tuple-element.10), channel_id=1, replica_groups=mesh['dp'=2,'mp'=16] {'dp'}, use_global_device_ids=true, to_apply=%region_2.3 | all-reduce | flops 512 | bytes 4096 | tf_op jit(solution)/shard_map/psum | solution.py:44
  142.8 0.6 broadcast_multiply_fusion.1
  143.4 185.8 %all-to-all-done = bf16[16,512,512]{2,1,0:T(8,128)(2,1)} async-done(((bf16[16,512,512]{2,1,0:T(8,128)(2,1)}), bf16[16,512,512]{2,1,0:T(8,128)(2,1)}, u32[]{:S(2)}, u32[]{:S(2)}) %all-to-all-start) | async-done | bytes 8388640 | tf_op jit(solution)/shard_map/all_to_all | solution.py:9
  329.2 12.3 %copy.10 = bf16[512,16,512]{0,2,1:T(8,128)(2,1)} copy(bf16[512,16,512]{2,0,1:T(8,128)(2,1)} %bitcast.1) | data formatting | bytes 16777216 | tf_op jit(solution)/shard_map/all_to_all | solution.py:9
  341.5 5.9 %fusion.7 = bf16[128,512]{1,0:T(8,128)(2,1)} fusion(bf16[128,8192]{1,0:T(8,128)(2,1)} %all-gather.2.cloned.1.call-done, bf16[512,8192]{0,1:T(8,128)(2,1)} %bitcast.8, bf16[128,512]{1,0:T(8,128)(2,1)S(1)} %copy-done.2), kind=kOutput, calls=%fused_computation.7 | convolution fusion | flops 1073938432 | bytes 10747904 | tf_op jit(solution)/shard_map/dot_general | solution.py:25
  347.4 7.8 %broadcast_multiply_fusion = f32[4096,512]{1,0:T(8,128)} fusion(f32[4096,512]{1,0:T(8,128)} %reduce-scatter.2.cloned.1.call-done), kind=kLoop, calls=%fused_computation | loop fusion | flops 2097152 | bytes 16777216 | tf_op jit(solution)/shard_map/mul | solution.py:34
  (39 shorter events, 0.4 us)
Async XLA Ops:
  8.0 79.6 %copy-start.1 = (bf16[128,512]{1,0:T(8,128)(2,1)S(1)}, bf16[128,512]{1,0:T(8,128)(2,1)}, u32[]{:S(2)}) copy-start(bf16[128,512]{1,0:T(8,128)(2,1)} %param.6) | copy-start | bytes 393220
  8.0 333.5 %all-gather.2.cloned.1.call-start = ((), (), s32[]{:S(2)}) async-start(), calls=%async_computation.2 | async-start | bytes 2228224 | tf_op jit(solution)/shard_map/all_gather | solution.py:26
  8.1 4.1 %collective-permute-start = (bf16[128,512]{1,0:T(8,128)(2,1)}, bf16[128,512]{1,0:T(8,128)(2,1)S(1)}, u32[]{:S(2)}, u32[]{:S(2)}) collective-permute-start(bf16[128,512]{1,0:T(8,128)(2,1)} %param.6), channel_id=1, source_target_pairs={{0,1},{1,2},{2,3},{3,4},{4,5},{5,6},{6,7},{7,8},{8,9},{9,10},{10,1... | collective-permute-start | bytes 393224 | tf_op jit(solution)/shard_map/ppermute | solution.py:14
  12.2 5.2 %collective-permute-start.1 = (bf16[128,512]{1,0:T(8,128)(2,1)S(1)}, bf16[128,512]{1,0:T(8,128)(2,1)S(1)}, u32[]{:S(2)}, u32[]{:S(2)}) collective-permute-start(bf16[128,512]{1,0:T(8,128)(2,1)S(1)} %collective-permute-done), channel_id=1, source_target_pairs={{0,1},{1,2},{2,3},{3,4},{4,5},{5,6},{6,7},{7,8},{8,9},{9,10},{10,1... | collective-permute-start | bytes 393224 | tf_op jit(solution)/shard_map/ppermute | solution.py:14
  17.4 5.3 %collective-permute-start.2 = (bf16[128,512]{1,0:T(8,128)(2,1)S(1)}, bf16[128,512]{1,0:T(8,128)(2,1)S(1)}, u32[]{:S(2)}, u32[]{:S(2)}) collective-permute-start(bf16[128,512]{1,0:T(8,128)(2,1)S(1)} %collective-permute-done.1), channel_id=1, source_target_pairs={{0,1},{1,2},{2,3},{3,4},{4,5},{5,6},{6,7},{7,8},{8,9},{9,10},{10,1... | collective-permute-start | bytes 393224 | tf_op jit(solution)/shard_map/ppermute | solution.py:14
  22.7 5.3 %collective-permute-start.3 = (bf16[128,512]{1,0:T(8,128)(2,1)S(1)}, bf16[128,512]{1,0:T(8,128)(2,1)S(1)}, u32[]{:S(2)}, u32[]{:S(2)}) collective-permute-start(bf16[128,512]{1,0:T(8,128)(2,1)S(1)} %collective-permute-done.2), channel_id=1, source_target_pairs={{0,1},{1,2},{2,3},{3,4},{4,5},{5,6},{6,7},{7,8},{8,9},{9,10},{10,1... | collective-permute-start | bytes 393224 | tf_op jit(solution)/shard_map/ppermute | solution.py:14
  27.9 5.3 %collective-permute-start.4 = (bf16[128,512]{1,0:T(8,128)(2,1)S(1)}, bf16[128,512]{1,0:T(8,128)(2,1)S(1)}, u32[]{:S(2)}, u32[]{:S(2)}) collective-permute-start(bf16[128,512]{1,0:T(8,128)(2,1)S(1)} %collective-permute-done.3), channel_id=1, source_target_pairs={{0,1},{1,2},{2,3},{3,4},{4,5},{5,6},{6,7},{7,8},{8,9},{9,10},{10,1... | collective-permute-start | bytes 393224 | tf_op jit(solution)/shard_map/ppermute | solution.py:14
  33.2 5.3 %collective-permute-start.5 = (bf16[128,512]{1,0:T(8,128)(2,1)S(1)}, bf16[128,512]{1,0:T(8,128)(2,1)S(1)}, u32[]{:S(2)}, u32[]{:S(2)}) collective-permute-start(bf16[128,512]{1,0:T(8,128)(2,1)S(1)} %collective-permute-done.4), channel_id=1, source_target_pairs={{0,1},{1,2},{2,3},{3,4},{4,5},{5,6},{6,7},{7,8},{8,9},{9,10},{10,1... | collective-permute-start | bytes 393224 | tf_op jit(solution)/shard_map/ppermute | solution.py:14
  38.5 5.3 %collective-permute-start.6 = (bf16[128,512]{1,0:T(8,128)(2,1)S(1)}, bf16[128,512]{1,0:T(8,128)(2,1)S(1)}, u32[]{:S(2)}, u32[]{:S(2)}) collective-permute-start(bf16[128,512]{1,0:T(8,128)(2,1)S(1)} %collective-permute-done.5), channel_id=1, source_target_pairs={{0,1},{1,2},{2,3},{3,4},{4,5},{5,6},{6,7},{7,8},{8,9},{9,10},{10,1... | collective-permute-start | bytes 393224 | tf_op jit(solution)/shard_map/ppermute | solution.py:14
  43.8 5.3 %collective-permute-start.7 = (bf16[128,512]{1,0:T(8,128)(2,1)S(1)}, bf16[128,512]{1,0:T(8,128)(2,1)S(1)}, u32[]{:S(2)}, u32[]{:S(2)}) collective-permute-start(bf16[128,512]{1,0:T(8,128)(2,1)S(1)} %collective-permute-done.6), channel_id=1, source_target_pairs={{0,1},{1,2},{2,3},{3,4},{4,5},{5,6},{6,7},{7,8},{8,9},{9,10},{10,1... | collective-permute-start | bytes 393224 | tf_op jit(solution)/shard_map/ppermute | solution.py:14
  49.1 5.3 %collective-permute-start.8 = (bf16[128,512]{1,0:T(8,128)(2,1)S(1)}, bf16[128,512]{1,0:T(8,128)(2,1)S(1)}, u32[]{:S(2)}, u32[]{:S(2)}) collective-permute-start(bf16[128,512]{1,0:T(8,128)(2,1)S(1)} %collective-permute-done.7), channel_id=1, source_target_pairs={{0,1},{1,2},{2,3},{3,4},{4,5},{5,6},{6,7},{7,8},{8,9},{9,10},{10,1... | collective-permute-start | bytes 393224 | tf_op jit(solution)/shard_map/ppermute | solution.py:14
  54.4 5.3 %collective-permute-start.9 = (bf16[128,512]{1,0:T(8,128)(2,1)S(1)}, bf16[128,512]{1,0:T(8,128)(2,1)S(1)}, u32[]{:S(2)}, u32[]{:S(2)}) collective-permute-start(bf16[128,512]{1,0:T(8,128)(2,1)S(1)} %collective-permute-done.8), channel_id=1, source_target_pairs={{0,1},{1,2},{2,3},{3,4},{4,5},{5,6},{6,7},{7,8},{8,9},{9,10},{10,1... | collective-permute-start | bytes 393224 | tf_op jit(solution)/shard_map/ppermute | solution.py:14
  59.7 5.3 %collective-permute-start.10 = (bf16[128,512]{1,0:T(8,128)(2,1)S(1)}, bf16[128,512]{1,0:T(8,128)(2,1)S(1)}, u32[]{:S(2)}, u32[]{:S(2)}) collective-permute-start(bf16[128,512]{1,0:T(8,128)(2,1)S(1)} %collective-permute-done.9), channel_id=1, source_target_pairs={{0,1},{1,2},{2,3},{3,4},{4,5},{5,6},{6,7},{7,8},{8,9},{9,10},{10,1... | collective-permute-start | bytes 393224 | tf_op jit(solution)/shard_map/ppermute | solution.py:14
  65.0 5.3 %collective-permute-start.11 = (bf16[128,512]{1,0:T(8,128)(2,1)S(1)}, bf16[128,512]{1,0:T(8,128)(2,1)S(1)}, u32[]{:S(2)}, u32[]{:S(2)}) collective-permute-start(bf16[128,512]{1,0:T(8,128)(2,1)S(1)} %collective-permute-done.10), channel_id=1, source_target_pairs={{0,1},{1,2},{2,3},{3,4},{4,5},{5,6},{6,7},{7,8},{8,9},{9,10},{10,1... | collective-permute-start | bytes 393224 | tf_op jit(solution)/shard_map/ppermute | solution.py:14
  70.3 5.3 %collective-permute-start.12 = (bf16[128,512]{1,0:T(8,128)(2,1)S(1)}, bf16[128,512]{1,0:T(8,128)(2,1)S(1)}, u32[]{:S(2)}, u32[]{:S(2)}) collective-permute-start(bf16[128,512]{1,0:T(8,128)(2,1)S(1)} %collective-permute-done.11), channel_id=1, source_target_pairs={{0,1},{1,2},{2,3},{3,4},{4,5},{5,6},{6,7},{7,8},{8,9},{9,10},{10,1... | collective-permute-start | bytes 393224 | tf_op jit(solution)/shard_map/ppermute | solution.py:14
  75.6 5.3 %collective-permute-start.13 = (bf16[128,512]{1,0:T(8,128)(2,1)S(1)}, bf16[128,512]{1,0:T(8,128)(2,1)S(1)}, u32[]{:S(2)}, u32[]{:S(2)}) collective-permute-start(bf16[128,512]{1,0:T(8,128)(2,1)S(1)} %collective-permute-done.12), channel_id=1, source_target_pairs={{0,1},{1,2},{2,3},{3,4},{4,5},{5,6},{6,7},{7,8},{8,9},{9,10},{10,1... | collective-permute-start | bytes 393224 | tf_op jit(solution)/shard_map/ppermute | solution.py:14
  80.9 5.3 %collective-permute-start.14 = (bf16[128,512]{1,0:T(8,128)(2,1)S(1)}, bf16[128,512]{1,0:T(8,128)(2,1)S(1)}, u32[]{:S(2)}, u32[]{:S(2)}) collective-permute-start(bf16[128,512]{1,0:T(8,128)(2,1)S(1)} %collective-permute-done.13), channel_id=1, source_target_pairs={{0,1},{1,2},{2,3},{3,4},{4,5},{5,6},{6,7},{7,8},{8,9},{9,10},{10,1... | collective-permute-start | bytes 393224 | tf_op jit(solution)/shard_map/ppermute | solution.py:14
  84.2 3.5 copy-start.2
  84.2 3.5 copy-start.3
  84.2 3.5 copy-start.4
  87.7 7.2 %copy-start = (bf16[128,16384]{1,0:T(8,128)(2,1)}, bf16[128,16384]{1,0:T(8,128)(2,1)S(1)}, u32[]{:S(2)}) copy-start(bf16[128,16384]{1,0:T(8,128)(2,1)S(1)} %constant_dynamic-update-slice_fusion) | copy-start | bytes 12582916
  94.9 252.6 %reduce-scatter.2.cloned.1.call-start = ((), (), s32[]{:S(2)}) async-start(), calls=%async_computation.3 | async-start | bytes 25165824 | tf_op jit(solution)/shard_map/reduce_scatter | solution.py:34
  104.7 224.6 %all-to-all-start = ((bf16[16,512,512]{2,1,0:T(8,128)(2,1)}), bf16[16,512,512]{2,1,0:T(8,128)(2,1)}, u32[]{:S(2)}, u32[]{:S(2)}) async-start(bf16[16,512,512]{2,1,0:T(8,128)(2,1)} %bitcast.7), calls=%async_computation | async-start | bytes 16777216 | tf_op jit(solution)/shard_map/all_to_all | solution.py:9
Sparse Core Ops, SparseCore 0:
  95.0 116.8 all-gather.1
Sparse Core Ops, SparseCore 1:
  104.8 213.7 reduce-scatter.1
